TPU v7x, 32 devices: a whole 2x2x4 slice. The times are simulated.
32 devices in a mesh: groups: 2 (over y), gx: 4 (over z), gy: 4 (over x, core).
Axes of the slice: x: 2, y: 2, z: 4, core: 2. Of those that a mesh axis runs over, the one named last changes fastest.
Arguments:
- thermal_deviation: float32 [32, 256, 512], P('groups', 'gy', 'gx'), parts along dimension 0, may hold values from -6 to 6
- brine_content: float32 [32, 256, 512], P('groups', 'gy', 'gx'), parts along dimension 0, may hold values from 0.2 to 2.4
- current_components: float32 [4, 16, 256, 512], P('groups', None, 'gy', 'gx'), parts along dimension 0, may hold values from -4 to 4
- sea_indicator: int32 [256, 512], P('gy', 'gx'), may hold values from 0 to 1, as said below
- flooded_layer_number: int32 [256, 512], P('gy', 'gx'), may hold values from 1 to 16
- footprint_square_metres: float32 [256, 512], P('gy', 'gx'), may hold values from 0.5 to 5
- rainfall_input: float32 [256, 512], P('gy', 'gx'), may hold values from -2 to 3.5
- seam_partner_index: int32 [512], P('gx'), may hold values from 0 to 511, as said below
Outputs:
- temperature_next: float32 [32, 256, 512], P('groups', 'gy', 'gx'), parts along dimension 0
- salinity_next: float32 [32, 256, 512], P('groups', 'gy', 'gx'), parts along dimension 0
There are 2 independent parts, one for each index of `groups`. A program takes and returns all parts, laid end to end along the dimension named above; an argument that names none is the same for every part. Nothing has to cross between parts.
Inputs may be any that keep to these rules, and one draw needn't show every extreme that they name: `sea_indicator`: at least one column is ocean. seam_partner_index[x] = (s - x) mod 512 for one s of each draw with s mod 128 = 127; the map is its own inverse and has no fixed point.
All inputs are finite; a program needn't handle non-finite values.
Results may differ from a plain program's by a relative error of at most 0.00002.
Values sent between devices are 32-bit elements; how exact they have to be, the bound alone decides.
A program may use at most 64 MiB of HBM per device.

v0:
```python
import jax
import jax.numpy as jnp
from jax import lax
from jax.sharding import PartitionSpec as P

time_step = 0.25
diffusivity = 0.5
vertical_mixing = 0.3
top_thickness = 0.5


def with_halo(cells, sides, width, closed):
    for axis, dim in sides:
        count = lax.axis_size(axis)
        ends = count if closed else count - 1
        head = lax.slice_in_dim(cells, 0, width, axis=dim)
        tail = lax.slice_in_dim(cells, cells.shape[dim] - width, cells.shape[dim], axis=dim)
        cells = jnp.concatenate(
            [
                lax.ppermute(tail, axis, [(i, (i + 1) % count) for i in range(ends)]),
                cells,
                lax.ppermute(head, axis, [((i + 1) % count, i) for i in range(ends)]),
            ],
            axis=dim,
        )
    return cells


def face_flux(near_cells, far_cells, face_speed, near_wet, far_wet):
    upwind = jnp.maximum(face_speed, 0.0) * near_cells + jnp.minimum(face_speed, 0.0) * far_cells
    return near_wet * far_wet * (upwind - diffusivity * (far_cells - near_cells))


def wet_from(depth_plane, layer_stack_number):
    level_index = jnp.arange(layer_stack_number, dtype=jnp.float32)
    return (level_index[:, None, None] < depth_plane[None]).astype(jnp.float32)


def split_tracer(block_planes, layer_stack_number):
    return block_planes[: 2 * layer_stack_number].reshape(
        (2, layer_stack_number) + block_planes.shape[1:]
    )


def shards(
    thermal_deviation,
    brine_content,
    current_components,
    sea_indicator,
    flooded_layer_number,
    footprint_square_metres,
    rainfall_input,
    seam_partner_index,
):
    layer_stack_number, parallel_total_number, meridian_total_number = thermal_deviation.shape
    stacked_layer_number = (sea_indicator * flooded_layer_number).astype(jnp.float32)
    wet_area = footprint_square_metres * sea_indicator.astype(jnp.float32)
    surface = brine_content[0]
    total_area, total_fresh, salt_fresh, salt_only = lax.psum(
        (
            jnp.sum(wet_area),
            jnp.sum(wet_area * rainfall_input),
            jnp.sum(wet_area * surface * rainfall_input),
            jnp.sum(wet_area * surface),
        ),
        ("gx", "gy"),
    )
    mean_fresh = total_fresh / total_area
    balanced = rainfall_input - mean_fresh
    total_salt = salt_fresh - mean_fresh * salt_only
    virtual = -surface * balanced + total_salt / total_area
    top_row = jnp.concatenate(
        [
            thermal_deviation[:, -1, :],
            brine_content[:, -1, :],
            current_components[1][:, -1, :],
            stacked_layer_number[-1:, :],
        ],
        axis=0,
    )
    gathered = lax.all_gather(top_row, "gx", axis=1, tiled=True)
    partner_row = jnp.take(gathered, seam_partner_index, axis=1)
    partner_fields = jnp.concatenate(
        [partner_row[: 2 * layer_stack_number], partner_row[3 * layer_stack_number :]], axis=0
    )
    partner_speed = partner_row[2 * layer_stack_number : 3 * layer_stack_number]
    is_top = lax.axis_index("gy") == lax.axis_size("gy") - 1
    planes = jnp.concatenate(
        [
            thermal_deviation,
            brine_content,
            current_components[0],
            current_components[1],
            stacked_layer_number[None],
        ],
        axis=0,
    )
    zonal_padded = with_halo(planes, (("gx", 2),), 1, True)
    meridional_padded = with_halo(planes, (("gy", 1),), 1, False)
    zonal_tracer = split_tracer(zonal_padded, layer_stack_number)
    zonal_wet = wet_from(zonal_padded[4 * layer_stack_number], layer_stack_number)
    zonal_near_speed = zonal_padded[2 * layer_stack_number : 3 * layer_stack_number][..., :-1]
    halo_top = jnp.concatenate(
        [
            meridional_padded[: 2 * layer_stack_number, -1, :],
            meridional_padded[4 * layer_stack_number :, -1, :],
        ],
        axis=0,
    )
    above_fields = jnp.where(is_top, partner_fields, halo_top)
    upper_tracer_cells = jnp.concatenate(
        [
            meridional_padded[: 2 * layer_stack_number, 1:-1, :],
            above_fields[: 2 * layer_stack_number, None, :],
        ],
        axis=1,
    )
    upper_depth = jnp.concatenate(
        [
            meridional_padded[4 * layer_stack_number, 1:-1, :],
            above_fields[2 * layer_stack_number][None, :],
        ],
        axis=0,
    )
    lower_cells = meridional_padded[:, :-1, :]
    lower_tracer = split_tracer(lower_cells, layer_stack_number)
    lower_wet = wet_from(lower_cells[4 * layer_stack_number], layer_stack_number)
    upper_tracer = split_tracer(upper_tracer_cells, layer_stack_number)
    upper_wet = wet_from(upper_depth, layer_stack_number)
    north_speed = lower_cells[3 * layer_stack_number : 4 * layer_stack_number]
    carried_quantity = jnp.stack([thermal_deviation, brine_content])
    wet_cells = wet_from(stacked_layer_number, layer_stack_number)
    zonal_flux = face_flux(
        zonal_tracer[..., :-1],
        zonal_tracer[..., 1:],
        zonal_near_speed,
        zonal_wet[..., :-1],
        zonal_wet[..., 1:],
    )
    fold_speed = 0.5 * (north_speed[:, -1, :] - partner_speed)
    last_speed = jnp.where(is_top, fold_speed, north_speed[:, -1, :])
    north_speed = jnp.concatenate([north_speed[:, :-1, :], last_speed[:, None, :]], axis=1)
    meridional_flux = face_flux(lower_tracer, upper_tracer, north_speed, lower_wet, upper_wet)
    vertical = (
        wet_cells[:-1]
        * wet_cells[1:]
        * vertical_mixing
        * (carried_quantity[:, :-1] - carried_quantity[:, 1:])
    )
    zero_layer = jnp.zeros_like(vertical[:, :1])
    from_above = jnp.concatenate([zero_layer, vertical], axis=1)
    to_below = jnp.concatenate([vertical, zero_layer], axis=1)
    tendency = time_step / footprint_square_metres * (
        zonal_flux[..., :-1]
        - zonal_flux[..., 1:]
        + meridional_flux[:, :, :-1]
        - meridional_flux[:, :, 1:]
    ) + time_step * (from_above - to_below)
    updated = carried_quantity + wet_cells * tendency
    surface_next = updated[1, 0] + time_step / top_thickness * virtual * wet_cells[0]
    salinity_next = jnp.concatenate([surface_next[None], updated[1, 1:]], axis=0)
    return (updated[0], salinity_next)


def solution(mesh):
    in_specs = (
        P("groups", "gy", "gx"),
        P("groups", "gy", "gx"),
        P("groups", None, "gy", "gx"),
        P("gy", "gx"),
        P("gy", "gx"),
        P("gy", "gx"),
        P("gy", "gx"),
        P("gx"),
    )
    out_specs = (P("groups", "gy", "gx"), P("groups", "gy", "gx"))
    return jax.shard_map(shards, mesh=mesh, in_specs=in_specs, out_specs=out_specs, check_vma=False)
```

profile of v0, /device:TPU:0, one launch (start us, length us, event | category | flops | bytes accessed | tf_op | source)
XLA Modules:
  0.0 111.4 jit_solution(16813490816440808588)
XLA Ops:
  0.6 2.3 %constant_dynamic-update-slice_fusion.2 = (f32[65,64,128]{2,0,1:T(8,128)S(1)}, f32[16,64,128]{2,0,1:T(8,128)}) fusion(f32[16,64,128]{2,1,0:T(8,128)} %param.8), kind=kLoop, calls=%fused_computation.82 | loop fusion | bytes 1572864
  2.9 0.1 fusion.26
  3.0 0.0 copy-start.5
  3.1 1.1 %constant_dynamic-update-slice_fusion.1 = (f32[65,64,128]{2,0,1:T(8,128)S(1)}, f32[16,64,128]{2,0,1:T(8,128)}) fusion(f32[65,64,128]{2,0,1:T(8,128)S(1)} %get-tuple-element.22, f32[16,64,128]{2,1,0:T(8,128)S(1)} %copy-done.2), kind=kLoop, calls=%fused_computation.81 | loop fusion | bytes 1572864
  4.2 0.3 fusion.10
  4.5 0.3 constant_dynamic-update-slice_fusion
  4.9 0.1 dynamic-update-slice.4
  5.0 2.9 %fusion.24 = (f32[65,64,1]{2,0,1:T(8,128)}, f32[65,64,1]{2,0,1:T(8,128)}) fusion(f32[65,64,128]{2,0,1:T(8,128)S(1)} %dynamic-update-slice.4), kind=kLoop, calls=%fused_computation.87 | loop fusion | bytes 66560 | tf_op jit(solution)/shard_map/slice | solution.py:17
  7.9 3.1 %copy.160 = f32[65,64,1]{0,1,2:T(8,128)} copy(f32[65,64,1]{2,0,1:T(8,128)} %get-tuple-element.14) | data formatting | bytes 33280 | tf_op jit(solution)/shard_map/slice | solution.py:17
  11.0 3.1 %collective-permute-start = (f32[65,64,1]{0,1,2:T(8,128)}, f32[65,64,1]{0,1,2:T(8,128)}, u32[]{:S(2)}, u32[]{:S(2)}) collective-permute-start(f32[65,64,1]{0,1,2:T(8,128)} %copy.160), channel_id=1, source_target_pairs={{0,4},{4,8},{8,12},{12,0},{1,5},{5,9},{9,13},{13,1},{2,6},{6,10},{... | collective-permute-start | bytes 49928 | tf_op jit(solution)/shard_map/ppermute | solution.py:20
  14.0 3.1 %copy.161 = f32[65,64,1]{0,1,2:T(8,128)} copy(f32[65,64,1]{2,0,1:T(8,128)} %get-tuple-element.15) | data formatting | bytes 33280 | tf_op jit(solution)/shard_map/slice | solution.py:16
  17.1 2.1 %collective-permute-start.1 = (f32[65,64,1]{0,1,2:T(8,128)}, f32[65,64,1]{0,1,2:T(8,128)}, u32[]{:S(2)}, u32[]{:S(2)}) collective-permute-start(f32[65,64,1]{0,1,2:T(8,128)} %copy.161), channel_id=1, source_target_pairs={{4,0},{8,4},{12,8},{0,12},{5,1},{9,5},{13,9},{1,13},{6,2},{10,6},{... | collective-permute-start | bytes 49928 | tf_op jit(solution)/shard_map/ppermute | solution.py:22
  19.2 0.6 fusion.25
  19.8 1.3 %collective-permute-start.2 = (f32[65,1,128]{2,0,1:T(8,128)}, f32[65,1,128]{2,0,1:T(8,128)}, u32[]{:S(2)}, u32[]{:S(2)}) collective-permute-start(f32[65,1,128]{2,0,1:T(8,128)} %get-tuple-element.17), channel_id=1, source_target_pairs={{1,0},{2,1},{3,2},{5,4},{6,5},{7,6},{9,8},{10,9},{11,10},{13,12},{... | collective-permute-start | bytes 99848 | tf_op jit(solution)/shard_map/ppermute | solution.py:22
  21.1 3.6 %collective-permute-start.3 = (f32[65,1,128]{2,0,1:T(8,128)}, f32[65,1,128]{2,0,1:T(8,128)}, u32[]{:S(2)}, u32[]{:S(2)}) collective-permute-start(f32[65,1,128]{2,0,1:T(8,128)} %get-tuple-element.16), channel_id=1, source_target_pairs={{0,1},{1,2},{2,3},{4,5},{5,6},{6,7},{8,9},{9,10},{10,11},{12,13},{... | collective-permute-start | bytes 99848 | tf_op jit(solution)/shard_map/ppermute | solution.py:20
  24.7 1.3 %copy.203 = f32[1,16,64,128]{3,1,2,0:T(8,128)S(1)} copy(f32[1,16,64,128]{3,2,1,0:T(8,128)} %copy-done.5) | data formatting | bytes 1048576
  26.1 0.7 compare_select_fusion
  26.8 0.5 compare_and_fusion
  27.3 1.1 pad_maximum_fusion.6
  28.4 0.8 fusion.11
  29.2 0.7 slice_bitcast_fusion.7
  29.9 0.7 slice_bitcast_fusion.5
  30.6 13.3 %all_gather.3 = f32[49,512]{1,0:T(8,128)S(1)} all-gather(f32[49,128]{1,0:T(8,128)S(1)} %pad_maximum_fusion.11), channel_id=1, replica_groups=mesh['groups'=2,'gx'=4,'gy'=4] {'gx'}, dimensions={1}, use_global_device_ids=true | all-gather | bytes 125440 | tf_op jit(solution)/shard_map/all_gather | solution.py:81
  43.9 0.8 copy.172
  44.8 0.7 pad_clamp_fusion
  45.4 1.6 %gather_fusion = f32[128,49]{1,0:T(8,128)S(1)} fusion(f32[49,512]{0,1:T(8,128)} %copy.172, s32[1024]{0:T(1024)S(1)} %pad_clamp_fusion), kind=kCustom, calls=%fused_computation | custom fusion | bytes 50688 | tf_op jit(solution)/shard_map/jit(_take)/gather | solution.py:82
  47.0 0.7 copy.173
  47.7 2.0 %fusion.12 = f32[15,64,128]{2,1,0:T(8,128)} fusion(f32[16,64,128]{2,1,0:T(8,128)} %fusion.11), kind=kLoop, calls=%fused_computation.45 | loop fusion | flops 245760 | bytes 1474560 | tf_op jit(solution)/shard_map/mul | solution.py:145
  49.8 0.8 convert_multiply_fusion
  50.6 1.4 %select_bitcast_fusion = f32[49,128]{1,0:T(8,128)} fusion(f32[128,49]{0,1:T(8,128)} %copy.173, pred[128]{0:T(512)(128)(4,1)} %compare_and_fusion), kind=kLoop, calls=%fused_computation.68 | loop fusion | flops 6272 | bytes 50304 | tf_op jit(solution)/shard_map/jit(_take)/select_n | solution.py:82
  51.9 0.7 fusion.22
  52.6 2.1 %fusion.7 = f32[2,15,64,128]{3,2,1,0:T(8,128)} fusion(f32[1,16,64,128]{3,2,1,0:T(8,128)S(1)} %bitcast.78, f32[1,16,64,128]{3,2,1,0:T(8,128)S(1)} %bitcast.76, f32[15,64,128]{2,1,0:T(8,128)} %fusion.12), kind=kLoop, calls=%fused_computation.26 | loop fusion | flops 983040 | bytes 2523136 | tf_op jit(solution)/shard_map/mul | solution.py:145
  54.7 0.7 fusion.19
  55.4 30.3 %all-reduce.2 = (f32[]{:T(128)}, f32[]{:T(128)}, f32[]{:T(128)}, f32[]{:T(128)}) all-reduce(f32[]{:T(128)} %get-tuple-element.3, f32[]{:T(128)} %get-tuple-element.4, f32[]{:T(128)} %get-tuple-element.5, f32[]{:T(128)} %get-tuple-element.2), channel_id=1, replica_groups=mesh['groups'=2,'gx'=4,'gy'=4] {'gx','gy'}, use_global_device_ids=true, to_apply=%region_5.0 | all-reduce | flops 4 | bytes 32 | tf_op jit(solution)/shard_map/psum | solution.py:59
  88.9 3.0 %copy.162 = f32[65,64,1]{2,0,1:T(8,128)} copy(f32[65,64,1]{0,1,2:T(8,128)} %collective-permute-done) | data formatting | bytes 33280 | tf_op jit(solution)/shard_map/ppermute | solution.py:20
  91.9 3.0 %copy.163 = f32[65,64,1]{2,0,1:T(8,128)} copy(f32[65,64,1]{0,1,2:T(8,128)} %collective-permute-done.1) | data formatting | bytes 33280 | tf_op jit(solution)/shard_map/ppermute | solution.py:22
  94.9 1.5 %pad_maximum_fusion.8 = f32[1,64,130]{2,0,1:T(1,128)S(1)} fusion(f32[65,64,1]{2,0,1:T(8,128)} %copy.163, f32[65,64,128]{2,0,1:T(8,128)S(1)} %dynamic-update-slice.4, f32[65,64,1]{2,0,1:T(8,128)} %copy.162), kind=kLoop, calls=%fused_computation.48 | loop fusion | flops 16640 | bytes 2196480 | tf_op jit(solution)/shard_map/slice | solution.py:101
  96.4 0.4 copy-done
  96.8 0.7 copy-done.1
  97.5 0.9 pad_maximum_fusion
  98.4 0.4 broadcast_maximum_fusion
  98.7 0.1 fusion.4
  98.9 0.3 slice_multiply_fusion
  99.2 1.2 %copy.167 = f32[32,64,130]{2,1,0:T(8,128)S(1)} copy(f32[32,64,130]{2,0,1:T(8,128)S(1)} %pad_maximum_fusion) | data formatting | bytes 2129920 | tf_op jit(solution)/shard_map/slice | solution.py:40
  100.4 0.1 broadcast_minimum_fusion
  100.5 0.6 copy.169
  101.1 0.6 copy.166
  101.8 1.1 subtract_multiply_fusion
  102.9 0.7 slice_bitcast_fusion.4
  103.6 0.7 slice_bitcast_fusion.8
  104.3 0.7 pad_maximum_fusion.10
  105.0 0.1 convert_select_fusion
  105.1 0.2 copy.174
  105.3 0.8 broadcast_maximum_fusion.1
  106.2 0.2 copy.177
  106.4 0.2 copy.175
  106.6 0.9 pad_maximum_fusion.4
  107.5 0.1 copy-done.6
  107.6 0.7 subtract_multiply_fusion.1
  108.3 0.3 copy-done.4
  108.6 0.3 copy-done.7
  109.0 0.7 fusion
  109.7 0.8 slice_bitcast_fusion
  110.6 0.8 pad_maximum_fusion.7
  (45 shorter events, 0.2 us)
Async XLA Ops:
  0.6 2.3 %copy-start.8 = (f32[2,16,64,128]{3,2,1,0:T(8,128)S(1)}, f32[2,16,64,128]{3,2,1,0:T(8,128)}, u32[]{:S(2)}) copy-start(f32[2,16,64,128]{3,2,1,0:T(8,128)} %param.10) | copy-start | bytes 3145732
  0.6 2.4 %copy-start.2 = (f32[16,64,128]{2,1,0:T(8,128)S(1)}, f32[16,64,128]{2,1,0:T(8,128)}, u32[]{:S(2)}) copy-start(f32[16,64,128]{2,1,0:T(8,128)} %param.9) | copy-start | bytes 1572868
  3.0 1.8 %copy-start.5 = (f32[1,16,64,128]{3,2,1,0:T(8,128)}, f32[1,16,64,128]{3,2,1,0:T(8,128)S(1)}, u32[]{:S(2)}) copy-start(f32[1,16,64,128]{3,2,1,0:T(8,128)S(1)} %get-tuple-element.19) | copy-start | bytes 1572868
  3.0 1.8 %copy-start.11 = (s32[64,128]{1,0:T(8,128)S(1)}, s32[64,128]{1,0:T(8,128)}, u32[]{:S(2)}) copy-start(s32[64,128]{1,0:T(8,128)} %param.11) | copy-start | bytes 98308
  3.0 1.8 %copy-start.13 = (s32[64,128]{1,0:T(8,128)S(1)}, s32[64,128]{1,0:T(8,128)}, u32[]{:S(2)}) copy-start(s32[64,128]{1,0:T(8,128)} %param.12) | copy-start | bytes 98308
  11.0 15.1 %copy-start.14 = (s32[128]{0:T(128)S(1)}, s32[128]{0:T(128)}, u32[]{:S(2)}) copy-start(s32[128]{0:T(128)} %param.15) | copy-start | bytes 1540
  11.0 16.3 %copy-start.3 = (f32[16,64,128]{2,1,0:T(8,128)S(1)}, f32[16,64,128]{2,1,0:T(8,128)}, u32[]{:S(2)}) copy-start(f32[16,64,128]{2,1,0:T(8,128)} %param.8) | copy-start | bytes 1572868
  11.0 77.9 %collective-permute-start = (f32[65,64,1]{0,1,2:T(8,128)}, f32[65,64,1]{0,1,2:T(8,128)}, u32[]{:S(2)}, u32[]{:S(2)}) collective-permute-start(f32[65,64,1]{0,1,2:T(8,128)} %copy.160), channel_id=1, source_target_pairs={{0,4},{4,8},{8,12},{12,0},{1,5},{5,9},{9,13},{13,1},{2,6},{6,10},{... | collective-permute-start | bytes 49928 | tf_op jit(solution)/shard_map/ppermute | solution.py:20
  17.1 74.8 %collective-permute-start.1 = (f32[65,64,1]{0,1,2:T(8,128)}, f32[65,64,1]{0,1,2:T(8,128)}, u32[]{:S(2)}, u32[]{:S(2)}) collective-permute-start(f32[65,64,1]{0,1,2:T(8,128)} %copy.161), channel_id=1, source_target_pairs={{4,0},{8,4},{12,8},{0,12},{5,1},{9,5},{13,9},{1,13},{6,2},{10,6},{... | collective-permute-start | bytes 49928 | tf_op jit(solution)/shard_map/ppermute | solution.py:22
  19.8 83.1 %collective-permute-start.2 = (f32[65,1,128]{2,0,1:T(8,128)}, f32[65,1,128]{2,0,1:T(8,128)}, u32[]{:S(2)}, u32[]{:S(2)}) collective-permute-start(f32[65,1,128]{2,0,1:T(8,128)} %get-tuple-element.17), channel_id=1, source_target_pairs={{1,0},{2,1},{3,2},{5,4},{6,5},{7,6},{9,8},{10,9},{11,10},{13,12},{... | collective-permute-start | bytes 99848 | tf_op jit(solution)/shard_map/ppermute | solution.py:22
  21.1 83.2 %collective-permute-start.3 = (f32[65,1,128]{2,0,1:T(8,128)}, f32[65,1,128]{2,0,1:T(8,128)}, u32[]{:S(2)}, u32[]{:S(2)}) collective-permute-start(f32[65,1,128]{2,0,1:T(8,128)} %get-tuple-element.16), channel_id=1, source_target_pairs={{0,1},{1,2},{2,3},{4,5},{5,6},{6,7},{8,9},{9,10},{10,11},{12,13},{... | collective-permute-start | bytes 99848 | tf_op jit(solution)/shard_map/ppermute | solution.py:20
  26.1 3.8 %copy-start.9 = (f32[1,16,64,128]{3,1,2,0:T(8,128)}, f32[1,16,64,128]{3,1,2,0:T(8,128)S(1)}, u32[]{:S(2)}) copy-start(f32[1,16,64,128]{3,1,2,0:T(8,128)S(1)} %copy.203) | copy-start | bytes 1572868
  47.7 7.0 %copy-start.10 = (f32[64,128]{1,0:T(8,128)S(1)}, f32[64,128]{1,0:T(8,128)}, u32[]{:S(2)}) copy-start(f32[64,128]{1,0:T(8,128)} %param.14) | copy-start | bytes 98308
  94.9 1.8 %copy-start = (f32[65,64,1]{2,0,1:T(8,128)S(1)}, f32[65,64,1]{2,0,1:T(8,128)}, u32[]{:S(2)}) copy-start(f32[65,64,1]{2,0,1:T(8,128)} %copy.162) | copy-start | bytes 49924
  94.9 2.5 %copy-start.1 = (f32[65,64,1]{2,0,1:T(8,128)S(1)}, f32[65,64,1]{2,0,1:T(8,128)}, u32[]{:S(2)}) copy-start(f32[65,64,1]{2,0,1:T(8,128)} %copy.163) | copy-start | bytes 49924
  101.8 2.5 %slice-start = ((f32[49,128]{1,0:T(8,128)}), f32[32,128]{1,0:T(8,128)S(1)}, s32[]{:S(2)}) async-start(f32[49,128]{1,0:T(8,128)} %select_bitcast_fusion), calls=%async_computation | async-start | bytes 32768 | tf_op jit(solution)/shard_map/slice | solution.py:84
  101.8 2.5 %slice-start.1 = ((f32[49,128]{1,0:T(8,128)}), f32[1,128]{1,0:T(1,128)S(1)}, s32[]{:S(2)}) async-start(f32[49,128]{1,0:T(8,128)} %select_bitcast_fusion), calls=%async_computation.1 | async-start | bytes 1024 | tf_op jit(solution)/shard_map/slice | solution.py:84
  104.3 1.1 copy-start.12
  106.4 1.2 %copy-start.6 = (f32[32,64,128]{2,1,0:T(8,128)S(1)}, f32[32,64,128]{2,1,0:T(8,128)}, u32[]{:S(2)}) copy-start(f32[32,64,128]{2,1,0:T(8,128)} %pad_maximum_fusion.6) | copy-start | bytes 3145732
  106.4 1.2 %slice-start.2 = ((f32[33,128]{1,0:T(8,128)}), f32[32,128]{1,0:T(8,128)S(1)}, s32[]{:S(2)}) async-start(f32[33,128]{1,0:T(8,128)} %copy-done.12), calls=%async_computation.2 | async-start | bytes 32768 | tf_op jit(solution)/shard_map/slice | solution.py:114
  107.6 1.0 copy-start.4
  107.6 1.4 %copy-start.7 = (f32[2,15,64,128]{3,2,1,0:T(8,128)S(1)}, f32[2,15,64,128]{3,2,1,0:T(8,128)}, u32[]{:S(2)}) copy-start(f32[2,15,64,128]{3,2,1,0:T(8,128)} %fusion.7) | copy-start | bytes 2949124
where the time goes:
time: 112 us; the launch traced here: 111 us
  blocking collectives  43.6 us (39%)
  local copies, waits for them, and re-layouts  32.9 us (29%)
  other arithmetic  20.6 us (18%)
  starting transfers between devices  10.1 us (9%)
  between operations  4.18 us (4%)
    psum x1, blocking collectives, shards(): lax.psum((jnp.sum(wet_area), jnp.sum(wet_area * rainfall_input), jnp.sum(...  30.3 us
    all_gather x1, blocking collectives, shards(): gathered = lax.all_gather(top_row, 'gx', axis=1, tiled=True)  13.3 us
    unnamed x37, local copies, waits for them, and re-layouts  7.21 us
    ppermute x2, starting transfers between devices, with_halo(): lax.ppermute(tail, axis, [(i, (i + 1) % count) for i in range(ends)])  6.7 us
    slice x3, local copies, waits for them, and re-layouts, with_halo(): lax.slice_in_dim(cells, cells.shape[dim] - width, cells.shape[dim], axis=...  6.57 us
    mul x2, other arithmetic, shards(): wet_cells[:-1] * wet_cells[1:] * vertical_mixing  4.14 us
    ppermute x2, starting transfers between devices, with_halo(): lax.ppermute(head, axis, [((i + 1) % count, i) for i in range(ends)])  3.37 us
    slice x1, local copies, waits for them, and re-layouts, with_halo(): head = lax.slice_in_dim(cells, 0, width, axis=dim)  3.07 us
  transfers between devices with their start and end apart: 4, of which 0 were waited for; matrix products, arithmetic and copies ran while one was open for 32% of the time, Pallas kernels for 0%

commit v1 on v0

--- a/solution.py
+++ b/solution.py
@@ -57,13 +57,16 @@
     wet_area = footprint_square_metres * sea_indicator.astype(jnp.float32)
     surface = brine_content[0]
     total_area, total_fresh, salt_fresh, salt_only = lax.psum(
-        (
-            jnp.sum(wet_area),
-            jnp.sum(wet_area * rainfall_input),
-            jnp.sum(wet_area * surface * rainfall_input),
-            jnp.sum(wet_area * surface),
+        lax.psum(
+            (
+                jnp.sum(wet_area),
+                jnp.sum(wet_area * rainfall_input),
+                jnp.sum(wet_area * surface * rainfall_input),
+                jnp.sum(wet_area * surface),
+            ),
+            "gy",
         ),
-        ("gx", "gy"),
+        "gx",
     )
     mean_fresh = total_fresh / total_area
     balanced = rainfall_input - mean_fresh

time: 112 us -> 99.8 us (0.89)
  blocking collectives: 43.6 us -> 30.9 us
    psum x1, blocking collectives: 30.3 us -> 6.34 us  [shards(): lax.psum((jnp.sum(wet_area), jnp.sum(wet_area * rainfall_input), jnp.sum(...]
    psum x0 -> x1, blocking collectives: none -> 11.2 us  [shards(): lax.psum(lax.psum((jnp.sum(wet_area), jnp.sum(wet_area * rainfall_input),...]
  transfers between devices with their start and end apart: 4 -> 4, of which waited for: 0 -> 0; matrix products, arithmetic and copies ran while one was open for 32% -> 36% of each run, Pallas kernels for 0% -> 0%
where the time goes in v1:
time: 99.8 us; the launch traced here: 98.7 us
  local copies, waits for them, and re-layouts  32.9 us (33%)
  blocking collectives  30.9 us (31%)
  other arithmetic  20.6 us (21%)
  starting transfers between devices  10.1 us (10%)
  between operations  4.25 us (4%)
    all_gather x1, blocking collectives, shards(): gathered = lax.all_gather(top_row, 'gx', axis=1, tiled=True)  13.3 us
    psum x1, blocking collectives, shards(): lax.psum(lax.psum((jnp.sum(wet_area), jnp.sum(wet_area * rainfall_input),...  11.2 us
    unnamed x37, local copies, waits for them, and re-layouts  7.2 us
    ppermute x2, starting transfers between devices, with_halo(): lax.ppermute(tail, axis, [(i, (i + 1) % count) for i in range(ends)])  6.7 us
    slice x3, local copies, waits for them, and re-layouts, with_halo(): lax.slice_in_dim(cells, cells.shape[dim] - width, cells.shape[dim], axis=...  6.56 us
    psum x1, blocking collectives, shards(): lax.psum((jnp.sum(wet_area), jnp.sum(wet_area * rainfall_input), jnp.sum(...  6.34 us
    mul x2, other arithmetic, shards(): wet_cells[:-1] * wet_cells[1:] * vertical_mixing  4.14 us
    ppermute x2, starting transfers between devices, with_halo(): lax.ppermute(head, axis, [((i + 1) % count, i) for i in range(ends)])  3.37 us
  transfers between devices with their start and end apart: 4, of which 0 were waited for; matrix products, arithmetic and copies ran while one was open for 36% of the time, Pallas kernels for 0%

profile of v1, /device:TPU:0, one launch (start us, length us, event | category | flops | bytes accessed | tf_op | source)
XLA Modules:
  0.0 98.7 jit_solution(15278288145174490555)
XLA Ops:
  0.6 2.3 %constant_dynamic-update-slice_fusion.2 = (f32[65,64,128]{2,0,1:T(8,128)S(1)}, f32[16,64,128]{2,0,1:T(8,128)}) fusion(f32[16,64,128]{2,1,0:T(8,128)} %param.8), kind=kLoop, calls=%fused_computation.82 | loop fusion | bytes 1572864
  2.9 0.1 fusion.26
  3.1 1.1 %constant_dynamic-update-slice_fusion.1 = (f32[65,64,128]{2,0,1:T(8,128)S(1)}, f32[16,64,128]{2,0,1:T(8,128)}) fusion(f32[65,64,128]{2,0,1:T(8,128)S(1)} %get-tuple-element.26, f32[16,64,128]{2,1,0:T(8,128)S(1)} %copy-done.2), kind=kLoop, calls=%fused_computation.81 | loop fusion | bytes 1572864
  4.2 0.3 fusion.10
  4.5 0.3 constant_dynamic-update-slice_fusion
  4.9 0.1 dynamic-update-slice.4
  5.0 2.9 %fusion.24 = (f32[65,64,1]{2,0,1:T(8,128)}, f32[65,64,1]{2,0,1:T(8,128)}) fusion(f32[65,64,128]{2,0,1:T(8,128)S(1)} %dynamic-update-slice.4), kind=kLoop, calls=%fused_computation.87 | loop fusion | bytes 66560 | tf_op jit(solution)/shard_map/slice | solution.py:17
  7.9 3.1 %copy.160 = f32[65,64,1]{0,1,2:T(8,128)} copy(f32[65,64,1]{2,0,1:T(8,128)} %get-tuple-element.18) | data formatting | bytes 33280 | tf_op jit(solution)/shard_map/slice | solution.py:17
  10.9 3.1 %collective-permute-start = (f32[65,64,1]{0,1,2:T(8,128)}, f32[65,64,1]{0,1,2:T(8,128)}, u32[]{:S(2)}, u32[]{:S(2)}) collective-permute-start(f32[65,64,1]{0,1,2:T(8,128)} %copy.160), channel_id=1, source_target_pairs={{0,4},{4,8},{8,12},{12,0},{1,5},{5,9},{9,13},{13,1},{2,6},{6,10},{... | collective-permute-start | bytes 49928 | tf_op jit(solution)/shard_map/ppermute | solution.py:20
  14.0 3.1 %copy.161 = f32[65,64,1]{0,1,2:T(8,128)} copy(f32[65,64,1]{2,0,1:T(8,128)} %get-tuple-element.19) | data formatting | bytes 33280 | tf_op jit(solution)/shard_map/slice | solution.py:16
  17.0 2.1 %collective-permute-start.1 = (f32[65,64,1]{0,1,2:T(8,128)}, f32[65,64,1]{0,1,2:T(8,128)}, u32[]{:S(2)}, u32[]{:S(2)}) collective-permute-start(f32[65,64,1]{0,1,2:T(8,128)} %copy.161), channel_id=1, source_target_pairs={{4,0},{8,4},{12,8},{0,12},{5,1},{9,5},{13,9},{1,13},{6,2},{10,6},{... | collective-permute-start | bytes 49928 | tf_op jit(solution)/shard_map/ppermute | solution.py:22
  19.1 0.6 fusion.25
  19.8 1.3 %collective-permute-start.2 = (f32[65,1,128]{2,0,1:T(8,128)}, f32[65,1,128]{2,0,1:T(8,128)}, u32[]{:S(2)}, u32[]{:S(2)}) collective-permute-start(f32[65,1,128]{2,0,1:T(8,128)} %get-tuple-element.21), channel_id=1, source_target_pairs={{1,0},{2,1},{3,2},{5,4},{6,5},{7,6},{9,8},{10,9},{11,10},{13,12},{... | collective-permute-start | bytes 99848 | tf_op jit(solution)/shard_map/ppermute | solution.py:22
  21.1 3.6 %collective-permute-start.3 = (f32[65,1,128]{2,0,1:T(8,128)}, f32[65,1,128]{2,0,1:T(8,128)}, u32[]{:S(2)}, u32[]{:S(2)}) collective-permute-start(f32[65,1,128]{2,0,1:T(8,128)} %get-tuple-element.20), channel_id=1, source_target_pairs={{0,1},{1,2},{2,3},{4,5},{5,6},{6,7},{8,9},{9,10},{10,11},{12,13},{... | collective-permute-start | bytes 99848 | tf_op jit(solution)/shard_map/ppermute | solution.py:20
  24.7 1.3 %copy.203 = f32[1,16,64,128]{3,1,2,0:T(8,128)S(1)} copy(f32[1,16,64,128]{3,2,1,0:T(8,128)} %copy-done.5) | data formatting | bytes 1048576
  26.1 0.6 compare_select_fusion
  26.7 0.5 compare_and_fusion
  27.3 1.1 %pad_maximum_fusion.6 = f32[32,64,128]{2,1,0:T(8,128)} fusion(f32[16,64,128]{2,1,0:T(8,128)S(1)} %copy-done.2, f32[16,64,128]{2,1,0:T(8,128)S(1)} %copy-done.3), kind=kLoop, calls=%fused_computation.21 | loop fusion | flops 262144 | bytes 2097152 | tf_op jit(solution)/shard_map/concatenate | solution.py:91
  28.3 0.8 fusion.11
  29.2 0.7 slice_bitcast_fusion.7
  29.9 0.7 slice_bitcast_fusion.5
  30.6 13.3 %all_gather.3 = f32[49,512]{1,0:T(8,128)S(1)} all-gather(f32[49,128]{1,0:T(8,128)S(1)} %pad_maximum_fusion.11), channel_id=1, replica_groups=mesh['groups'=2,'gx'=4,'gy'=4] {'gx'}, dimensions={1}, use_global_device_ids=true | all-gather | bytes 125440 | tf_op jit(solution)/shard_map/all_gather | solution.py:84
  43.9 0.8 copy.172
  44.7 0.6 pad_clamp_fusion
  45.4 1.6 %gather_fusion = f32[128,49]{1,0:T(8,128)S(1)} fusion(f32[49,512]{0,1:T(8,128)} %copy.172, s32[1024]{0:T(1024)S(1)} %pad_clamp_fusion), kind=kCustom, calls=%fused_computation | custom fusion | bytes 50688 | tf_op jit(solution)/shard_map/jit(_take)/gather | solution.py:85
  47.0 0.7 copy.173
  47.7 2.0 %fusion.12 = f32[15,64,128]{2,1,0:T(8,128)} fusion(f32[16,64,128]{2,1,0:T(8,128)} %fusion.11), kind=kLoop, calls=%fused_computation.45 | loop fusion | flops 245760 | bytes 1474560 | tf_op jit(solution)/shard_map/mul | solution.py:148
  49.7 0.8 convert_multiply_fusion
  50.5 1.4 %select_bitcast_fusion = f32[49,128]{1,0:T(8,128)} fusion(f32[128,49]{0,1:T(8,128)} %copy.173, pred[128]{0:T(512)(128)(4,1)} %compare_and_fusion), kind=kLoop, calls=%fused_computation.68 | loop fusion | flops 6272 | bytes 50304 | tf_op jit(solution)/shard_map/jit(_take)/select_n | solution.py:85
  51.9 0.7 fusion.22
  52.6 2.1 %fusion.7 = f32[2,15,64,128]{3,2,1,0:T(8,128)} fusion(f32[1,16,64,128]{3,2,1,0:T(8,128)S(1)} %bitcast.78, f32[1,16,64,128]{3,2,1,0:T(8,128)S(1)} %bitcast.76, f32[15,64,128]{2,1,0:T(8,128)} %fusion.12), kind=kLoop, calls=%fused_computation.26 | loop fusion | flops 983040 | bytes 2523136 | tf_op jit(solution)/shard_map/mul | solution.py:148
  54.7 0.7 fusion.19
  55.4 6.3 %all-reduce.2 = (f32[]{:T(128)}, f32[]{:T(128)}, f32[]{:T(128)}, f32[]{:T(128)}) all-reduce(f32[]{:T(128)} %get-tuple-element.3, f32[]{:T(128)} %get-tuple-element.4, f32[]{:T(128)} %get-tuple-element.5, f32[]{:T(128)} %get-tuple-element.2), channel_id=1, replica_groups=mesh['groups'=2,'gx'=4,'gy'=4] {'gy'}, use_global_device_ids=true, to_apply=%region_7.0 | all-reduce | flops 4 | bytes 32 | tf_op jit(solution)/shard_map/psum | solution.py:60
  61.7 11.2 %all-reduce.3 = (f32[]{:T(128)}, f32[]{:T(128)}, f32[]{:T(128)}, f32[]{:T(128)}) all-reduce(f32[]{:T(128)} %get-tuple-element.6, f32[]{:T(128)} %get-tuple-element.7, f32[]{:T(128)} %get-tuple-element.8, f32[]{:T(128)} %get-tuple-element.9), channel_id=1, replica_groups=mesh['groups'=2,'gx'=4,'gy'=4] {'gx'}, use_global_device_ids=true, to_apply=%region_8.0 | all-reduce | flops 4 | bytes 32 | tf_op jit(solution)/shard_map/psum | solution.py:59
  76.2 3.0 %copy.162 = f32[65,64,1]{2,0,1:T(8,128)} copy(f32[65,64,1]{0,1,2:T(8,128)} %collective-permute-done) | data formatting | bytes 33280 | tf_op jit(solution)/shard_map/ppermute | solution.py:20
  79.2 3.0 %copy.163 = f32[65,64,1]{2,0,1:T(8,128)} copy(f32[65,64,1]{0,1,2:T(8,128)} %collective-permute-done.1) | data formatting | bytes 33280 | tf_op jit(solution)/shard_map/ppermute | solution.py:22
  82.2 1.5 %pad_maximum_fusion.8 = f32[1,64,130]{2,0,1:T(1,128)S(1)} fusion(f32[65,64,1]{2,0,1:T(8,128)} %copy.163, f32[65,64,128]{2,0,1:T(8,128)S(1)} %dynamic-update-slice.4, f32[65,64,1]{2,0,1:T(8,128)} %copy.162), kind=kLoop, calls=%fused_computation.48 | loop fusion | flops 16640 | bytes 2196480 | tf_op jit(solution)/shard_map/slice | solution.py:104
  83.6 0.4 copy-done
  84.0 0.7 copy-done.1
  84.7 0.9 pad_maximum_fusion
  85.6 0.4 broadcast_maximum_fusion
  86.0 0.1 fusion.4
  86.1 0.3 slice_multiply_fusion
  86.5 1.2 %copy.167 = f32[32,64,130]{2,1,0:T(8,128)S(1)} copy(f32[32,64,130]{2,0,1:T(8,128)S(1)} %pad_maximum_fusion) | data formatting | bytes 2129920 | tf_op jit(solution)/shard_map/slice | solution.py:40
  87.7 0.1 broadcast_minimum_fusion
  87.8 0.6 copy.169
  88.4 0.6 copy.166
  89.0 1.1 %subtract_multiply_fusion = f32[2,16,64,129]{3,2,1,0:T(8,128)S(1)} fusion(f32[2,16,64,130]{3,2,1,0:T(8,128)S(1)} %bitcast.75, f32[16,64,129]{2,1,0:T(8,128)S(1)} %copy.169, f32[16,64,129]{2,1,0:T(8,128)S(1)} %copy.166, f32[16,64,129]{2,1,0:T(8,128)S(1)} %slice_multiply_fusion), kind=kLoop, calls=%fused_computation.3 | loop fusion | flops 1849344 | bytes 4755456 | tf_op jit(solution)/shard_map/mul | solution.py:31
  90.1 0.7 slice_bitcast_fusion.4
  90.8 0.7 slice_bitcast_fusion.8
  91.6 0.7 pad_maximum_fusion.10
  92.3 0.1 convert_select_fusion
  92.4 0.2 copy.174
  92.6 0.8 broadcast_maximum_fusion.1
  93.4 0.2 copy.177
  93.6 0.2 copy.175
  93.8 0.9 pad_maximum_fusion.4
  94.8 0.1 copy-done.6
  94.9 0.7 subtract_multiply_fusion.1
  95.6 0.3 copy-done.4
  95.9 0.3 copy-done.7
  96.2 0.7 fusion
  97.0 0.8 slice_bitcast_fusion
  97.8 0.8 pad_maximum_fusion.7
  (46 shorter events, 0.2 us)
Async XLA Ops:
  0.6 2.3 %copy-start.8 = (f32[2,16,64,128]{3,2,1,0:T(8,128)S(1)}, f32[2,16,64,128]{3,2,1,0:T(8,128)}, u32[]{:S(2)}) copy-start(f32[2,16,64,128]{3,2,1,0:T(8,128)} %param.10) | copy-start | bytes 3145732
  0.6 2.4 %copy-start.2 = (f32[16,64,128]{2,1,0:T(8,128)S(1)}, f32[16,64,128]{2,1,0:T(8,128)}, u32[]{:S(2)}) copy-start(f32[16,64,128]{2,1,0:T(8,128)} %param.9) | copy-start | bytes 1572868
  3.0 1.8 %copy-start.5 = (f32[1,16,64,128]{3,2,1,0:T(8,128)}, f32[1,16,64,128]{3,2,1,0:T(8,128)S(1)}, u32[]{:S(2)}) copy-start(f32[1,16,64,128]{3,2,1,0:T(8,128)S(1)} %get-tuple-element.23) | copy-start | bytes 1572868
  3.0 1.8 %copy-start.11 = (s32[64,128]{1,0:T(8,128)S(1)}, s32[64,128]{1,0:T(8,128)}, u32[]{:S(2)}) copy-start(s32[64,128]{1,0:T(8,128)} %param.11) | copy-start | bytes 98308
  3.0 1.8 %copy-start.13 = (s32[64,128]{1,0:T(8,128)S(1)}, s32[64,128]{1,0:T(8,128)}, u32[]{:S(2)}) copy-start(s32[64,128]{1,0:T(8,128)} %param.12) | copy-start | bytes 98308
  10.9 15.2 %copy-start.14 = (s32[128]{0:T(128)S(1)}, s32[128]{0:T(128)}, u32[]{:S(2)}) copy-start(s32[128]{0:T(128)} %param.15) | copy-start | bytes 1540
  10.9 16.3 %copy-start.3 = (f32[16,64,128]{2,1,0:T(8,128)S(1)}, f32[16,64,128]{2,1,0:T(8,128)}, u32[]{:S(2)}) copy-start(f32[16,64,128]{2,1,0:T(8,128)} %param.8) | copy-start | bytes 1572868
  10.9 65.2 %collective-permute-start = (f32[65,64,1]{0,1,2:T(8,128)}, f32[65,64,1]{0,1,2:T(8,128)}, u32[]{:S(2)}, u32[]{:S(2)}) collective-permute-start(f32[65,64,1]{0,1,2:T(8,128)} %copy.160), channel_id=1, source_target_pairs={{0,4},{4,8},{8,12},{12,0},{1,5},{5,9},{9,13},{13,1},{2,6},{6,10},{... | collective-permute-start | bytes 49928 | tf_op jit(solution)/shard_map/ppermute | solution.py:20
  17.0 62.1 %collective-permute-start.1 = (f32[65,64,1]{0,1,2:T(8,128)}, f32[65,64,1]{0,1,2:T(8,128)}, u32[]{:S(2)}, u32[]{:S(2)}) collective-permute-start(f32[65,64,1]{0,1,2:T(8,128)} %copy.161), channel_id=1, source_target_pairs={{4,0},{8,4},{12,8},{0,12},{5,1},{9,5},{13,9},{1,13},{6,2},{10,6},{... | collective-permute-start | bytes 49928 | tf_op jit(solution)/shard_map/ppermute | solution.py:22
  19.8 70.3 %collective-permute-start.2 = (f32[65,1,128]{2,0,1:T(8,128)}, f32[65,1,128]{2,0,1:T(8,128)}, u32[]{:S(2)}, u32[]{:S(2)}) collective-permute-start(f32[65,1,128]{2,0,1:T(8,128)} %get-tuple-element.21), channel_id=1, source_target_pairs={{1,0},{2,1},{3,2},{5,4},{6,5},{7,6},{9,8},{10,9},{11,10},{13,12},{... | collective-permute-start | bytes 99848 | tf_op jit(solution)/shard_map/ppermute | solution.py:22
  21.1 70.5 %collective-permute-start.3 = (f32[65,1,128]{2,0,1:T(8,128)}, f32[65,1,128]{2,0,1:T(8,128)}, u32[]{:S(2)}, u32[]{:S(2)}) collective-permute-start(f32[65,1,128]{2,0,1:T(8,128)} %get-tuple-element.20), channel_id=1, source_target_pairs={{0,1},{1,2},{2,3},{4,5},{5,6},{6,7},{8,9},{9,10},{10,11},{12,13},{... | collective-permute-start | bytes 99848 | tf_op jit(solution)/shard_map/ppermute | solution.py:20
  26.1 3.8 %copy-start.9 = (f32[1,16,64,128]{3,1,2,0:T(8,128)}, f32[1,16,64,128]{3,1,2,0:T(8,128)S(1)}, u32[]{:S(2)}) copy-start(f32[1,16,64,128]{3,1,2,0:T(8,128)S(1)} %copy.203) | copy-start | bytes 1572868
  47.7 7.0 %copy-start.10 = (f32[64,128]{1,0:T(8,128)S(1)}, f32[64,128]{1,0:T(8,128)}, u32[]{:S(2)}) copy-start(f32[64,128]{1,0:T(8,128)} %param.14) | copy-start | bytes 98308
  82.2 1.8 %copy-start = (f32[65,64,1]{2,0,1:T(8,128)S(1)}, f32[65,64,1]{2,0,1:T(8,128)}, u32[]{:S(2)}) copy-start(f32[65,64,1]{2,0,1:T(8,128)} %copy.162) | copy-start | bytes 49924
  82.2 2.5 %copy-start.1 = (f32[65,64,1]{2,0,1:T(8,128)S(1)}, f32[65,64,1]{2,0,1:T(8,128)}, u32[]{:S(2)}) copy-start(f32[65,64,1]{2,0,1:T(8,128)} %copy.163) | copy-start | bytes 49924
  89.0 2.5 %slice-start = ((f32[49,128]{1,0:T(8,128)}), f32[32,128]{1,0:T(8,128)S(1)}, s32[]{:S(2)}) async-start(f32[49,128]{1,0:T(8,128)} %select_bitcast_fusion), calls=%async_computation | async-start | bytes 32768 | tf_op jit(solution)/shard_map/slice | solution.py:87
  89.0 2.5 %slice-start.1 = ((f32[49,128]{1,0:T(8,128)}), f32[1,128]{1,0:T(1,128)S(1)}, s32[]{:S(2)}) async-start(f32[49,128]{1,0:T(8,128)} %select_bitcast_fusion), calls=%async_computation.1 | async-start | bytes 1024 | tf_op jit(solution)/shard_map/slice | solution.py:87
  91.5 1.1 %copy-start.12 = (f32[33,128]{1,0:T(8,128)}, f32[33,128]{1,0:T(8,128)S(1)}, u32[]{:S(2)}) copy-start(f32[33,128]{1,0:T(8,128)S(1)} %maximum_select_fusion) | copy-start | bytes 50692
  93.6 1.2 %copy-start.6 = (f32[32,64,128]{2,1,0:T(8,128)S(1)}, f32[32,64,128]{2,1,0:T(8,128)}, u32[]{:S(2)}) copy-start(f32[32,64,128]{2,1,0:T(8,128)} %pad_maximum_fusion.6) | copy-start | bytes 3145732
  93.6 1.2 %slice-start.2 = ((f32[33,128]{1,0:T(8,128)}), f32[32,128]{1,0:T(8,128)S(1)}, s32[]{:S(2)}) async-start(f32[33,128]{1,0:T(8,128)} %copy-done.12), calls=%async_computation.2 | async-start | bytes 32768 | tf_op jit(solution)/shard_map/slice | solution.py:117
  94.9 1.0 %copy-start.4 = (f32[16,64,128]{2,1,0:T(8,128)S(1)}, f32[16,64,128]{2,1,0:T(8,128)}, u32[]{:S(2)}) copy-start(f32[16,64,128]{2,1,0:T(8,128)} %fusion.11) | copy-start | bytes 1572868
  94.9 1.4 %copy-start.7 = (f32[2,15,64,128]{3,2,1,0:T(8,128)S(1)}, f32[2,15,64,128]{3,2,1,0:T(8,128)}, u32[]{:S(2)}) copy-start(f32[2,15,64,128]{3,2,1,0:T(8,128)} %fusion.7) | copy-start | bytes 2949124
